TPU v7x, 128 devices: a whole 4x4x4 slice. The times are simulated.
128 devices in a mesh: dp: 8 (over x, core), crop: 4 (over y), tensor: 4 (over z).
Axes of the slice: x: 4, y: 4, z: 4, core: 2. Of those that a mesh axis runs over, the one named last changes fastest.
Arguments:
- hidden_a: bfloat16 [2048, 8192], P('crop', 'dp'), as said below
- hidden_b: bfloat16 [2048, 8192], P('crop', 'dp'), as said below
- weight: bfloat16 [8192, 8192], P('dp', 'tensor')
Outputs:
- weight_grad: float32 [8192, 8192], P(('dp', 'crop'), 'tensor')
Inputs may be any that keep to these rules, and one draw needn't show every extreme that they name: `hidden_a`: nonnegative entries. `hidden_b`: nonnegative entries.
All inputs are finite; a program needn't handle non-finite values.
Results may differ from a plain program's by a relative error of at most 0.0015.
Values may be sent and summed in bfloat16 or wider, within the bound.
A program may use at most 128 MiB of HBM per device.

v0:
```python
import jax
import jax.numpy as jnp
from jax import lax
from jax.sharding import PartitionSpec as P

epsilon = 0.0001


def sent_to_all(array, axis):
    peers = lax.axis_size(axis)
    return lax.all_to_all(
        jnp.broadcast_to(array[None], (peers, *array.shape)), axis, 0, 0, tiled=True
    )


def over_copies(array, axis):
    return sent_to_all(array, axis).sum(axis=0)


def body(hidden_a, hidden_b, weight):
    group_size = lax.axis_size(("dp", "crop"))
    data_count = lax.axis_size("dp")
    block_rows = hidden_a.shape[0]
    local_rows = block_rows // data_count
    total_rows = local_rows * group_size
    left_part = jnp.dot(hidden_a, weight, preferred_element_type=jnp.float32)
    right_part = jnp.dot(hidden_b, weight, preferred_element_type=jnp.float32)
    joined = lax.psum_scatter(
        jnp.stack([left_part, right_part], axis=1), "dp", scatter_dimension=0, tiled=True
    ).astype(jnp.bfloat16)
    stacked = jnp.stack([joined[:, 0, :], joined[:, 1, :]]).astype(jnp.float32)
    col_means = over_copies(jnp.sum(stacked, axis=1), ("dp", "crop")) / total_rows
    centered = stacked - col_means[:, None, :]
    spread = over_copies(jnp.sum(centered * centered, axis=1), ("dp", "crop"))
    deviation = jnp.sqrt(spread / (total_rows - 1.0) + epsilon)
    rounded = centered.astype(jnp.bfloat16)
    everyone = lax.all_gather(rounded, ("dp", "crop"), axis=1, tiled=True)
    gram = jnp.einsum("vrf,vbf->vrb", rounded, everyone, preferred_element_type=jnp.float32)
    gram = over_copies(gram, "tensor")
    gram_low = gram.astype(jnp.bfloat16)
    products = jnp.einsum("vrb,vbf->vrf", gram_low, everyone, preferred_element_type=jnp.float32)
    hinge_rate = jnp.where(deviation < 1.0, 25.0 / ((total_rows - 1.0) * deviation), 0.0)[
        :, None, :
    ]
    differ = stacked[0] - stacked[1]
    pull_term = jnp.stack([differ, -differ]) * (50.0 / total_rows)
    cov_scale = 4.0 / (total_rows - 1.0) ** 2
    row_grads = (
        pull_term - hinge_rate * centered + cov_scale * (products - centered * spread[:, None, :])
    )
    row_grads = row_grads.astype(jnp.bfloat16)
    block_grads = lax.all_gather(row_grads, "dp", axis=1, tiled=True)
    across = (((0,), (0,)), ((), ()))
    left_part = lax.dot_general(
        hidden_a, block_grads[0], across, preferred_element_type=jnp.float32
    )
    right_part = lax.dot_general(
        hidden_b, block_grads[1], across, preferred_element_type=jnp.float32
    )
    return lax.psum_scatter(left_part + right_part, "crop", scatter_dimension=0, tiled=True)


def solution(mesh):
    placed = (P("crop", "dp"), P("crop", "dp"), P("dp", "tensor"))
    return jax.shard_map(
        body, mesh=mesh, in_specs=placed, out_specs=P(("dp", "crop"), "tensor"), check_vma=False
    )
```

profile of v0, /device:TPU:1, one launch (start us, length us, event | category | flops | bytes accessed | tf_op | source)
XLA Modules:
  0.0 376.3 jit_solution(18045313686721249146)
XLA Ops:
  6.5 0.0 copy-start
  6.5 0.0 reduce-scatter.3.cloned.1.call-start
  6.5 0.0 copy-start.4
  6.5 5.0 %convolution_bitcast_fusion = f32[512,1,2048]{2,0,1:T(8,128)S(1)} fusion(bf16[512,1024]{1,0:T(8,128)(2,1)} %param.4, bf16[1024,2048]{1,0:T(8,128)(2,1)} %param.5), kind=kOutput, calls=%fused_computation.2 | convolution fusion | flops 2147483648 | bytes 9437184 | tf_op jit(solution)/shard_map/dot_general | solution.py:27
  11.5 0.0 copy-done
  11.5 0.0 copy-done.4
  11.6 2.4 convolution_bitcast_fusion.1
  13.9 3.8 %pad_maximum_fusion = f32[512,2,2048]{2,0,1:T(8,128)} fusion(f32[512,1,2048]{2,0,1:T(8,128)S(1)} %convolution_bitcast_fusion, f32[512,1,2048]{2,0,1:T(8,128)S(1)} %convolution_bitcast_fusion.1), kind=kLoop, calls=%fused_computation | loop fusion | flops 2097152 | bytes 16777216 | tf_op jit(solution)/shard_map/stack | solution.py:29
  17.7 0.0 reduce-scatter.3.cloned.1.call-update
  17.7 0.0 all-gather.3.cloned.1.call-start
  17.8 55.2 %reduce-scatter.3.cloned.1.call-done = f32[64,2,2048]{2,0,1:T(8,128)} async-done(((f32[512,2,2048]{2,0,1:T(8,128)}), f32[64,2,2048]{2,0,1:T(8,128)}) %reduce-scatter.3.cloned.1.call-update) | async-done | bytes 1048592 | tf_op jit(solution)/shard_map/reduce_scatter | solution.py:28
  73.0 1.3 convert_element_type.15
  74.3 0.1 convert_reduce_fusion
  74.4 0.2 broadcast_in_dim.9
  74.7 17.3 %all_to_all.15 = f32[32,2,2048]{2,1,0:T(2,128)S(1)} all-to-all(f32[32,2,2048]{2,1,0:T(2,128)S(1)} %broadcast_in_dim.9), channel_id=1, replica_groups=mesh['dp'=8,'crop'=4,'tensor'=4] {'dp','crop'}, dimensions={0} | all-to-all | bytes 1048576 | tf_op jit(solution)/shard_map/all_to_all | solution.py:11
  92.0 0.2 reduce_sum.46
  92.1 1.0 multiply_reduce_fusion
  93.1 0.0 all-gather.3.cloned.1.call-update
  93.1 1.0 broadcast_in_dim.10
  94.2 4.5 %all-to-all-start.1 = ((f32[32,2,2048]{2,1,0:T(2,128)}), f32[32,2,2048]{2,1,0:T(2,128)S(1)}, u32[]{:S(2)}, u32[]{:S(2)}) async-start(f32[32,2,2048]{2,1,0:T(2,128)} %broadcast_in_dim.10), calls=%async_computation.2 | async-start | bytes 1048576 | tf_op jit(solution)/shard_map/all_to_all | solution.py:11
  98.6 67.9 %all-gather.3.cloned.1.call-done = bf16[2,2048,2048]{2,1,0:T(8,128)(2,1)} async-done(((bf16[2,64,2048]{2,1,0:T(8,128)(2,1)}), bf16[2,2048,2048]{2,1,0:T(8,128)(2,1)}) %all-gather.3.cloned.1.call-update) | async-done | bytes 16777232 | tf_op jit(solution)/shard_map/all_gather | solution.py:37
  166.5 11.1 %fusion.8 = f32[2,64,2048]{2,1,0:T(8,128)S(1)} fusion(bf16[2,64,2048]{2,1,0:T(8,128)(2,1)} %get-tuple-element.8, bf16[2,2048,2048]{2,1,0:T(8,128)(2,1)} %all-gather.3.cloned.1.call-done), kind=kOutput, calls=%fused_computation.25 | convolution fusion | flops 1073741824 | bytes 18350080 | tf_op jit(solution)/shard_map/vrf,vbf->vrb/dot_general | solution.py:38
  177.6 0.0 all-to-all-done.1
  177.6 2.6 broadcast_in_dim.12
  180.2 4.8 %all-to-all-start.2 = ((f32[4,2,64,2048]{3,2,1,0:T(8,128)}), f32[4,2,64,2048]{3,2,1,0:T(8,128)}, u32[]{:S(2)}, u32[]{:S(2)}) async-start(f32[4,2,64,2048]{3,2,1,0:T(8,128)} %broadcast_in_dim.12), calls=%async_computation.3 | async-start | bytes 8388608 | tf_op jit(solution)/shard_map/all_to_all | solution.py:11
  185.0 0.2 all-gather.5.cloned.1.call-start
  185.3 0.1 fusion.6
  185.3 0.9 fusion.7
  186.2 0.2 reduce_sum.48
  186.4 0.0 copy-start.2
  186.5 47.3 %all-to-all-done.2 = f32[4,2,64,2048]{3,2,1,0:T(8,128)} async-done(((f32[4,2,64,2048]{3,2,1,0:T(8,128)}), f32[4,2,64,2048]{3,2,1,0:T(8,128)}, u32[]{:S(2)}, u32[]{:S(2)}) %all-to-all-start.2) | async-done | bytes 4194336 | tf_op jit(solution)/shard_map/all_to_all | solution.py:11
  233.7 2.6 reduce_sum.49
  236.3 0.0 copy-done.2
  236.4 9.8 %fusion.2 = bf16[2,64,2048]{2,1,0:T(8,128)(2,1)} fusion(bf16[2,2048,2048]{2,1,0:T(8,128)(2,1)} %all-gather.3.cloned.1.call-done, f32[1,64,2048]{2,1,0:T(8,128)S(1)} %get-tuple-element.5, f32[1,64,2048]{2,1,0:T(8,128)S(1)} %copy-done.2, f32[2,2048]{1,0:T(2,128)S(1)} %reduce_sum.48, bf16[2,64,2048]{2,1,0:T(8,128)(2,1)S(1)} %reduce_sum.49, ...), kind=kOutput, calls=%fused_computation.7 | convolution fusion | flops 1076887552 | bytes 19447808 | tf_op jit(solution)/shard_map/vrb,vbf->vrf/dot_general | solution.py:41
  246.1 0.0 all-gather.5.cloned.1.call-update
  246.1 0.0 copy-start.3
  246.2 0.0 reduce-scatter.5.cloned.1.call-start
  246.2 30.5 %all-gather.5.cloned.1.call-done = bf16[2,512,2048]{2,1,0:T(8,128)(2,1)} async-done(((bf16[2,64,2048]{2,1,0:T(8,128)(2,1)}), bf16[2,512,2048]{2,1,0:T(8,128)(2,1)}) %all-gather.5.cloned.1.call-update) | async-done | bytes 4194320 | tf_op jit(solution)/shard_map/all_gather | solution.py:52
  276.7 0.0 copy-start.1
  276.7 4.1 %fusion.3 = f32[2048,1024]{1,0:T(8,128)S(1)} fusion(bf16[512,1024]{1,0:T(8,128)(2,1)S(1)} %copy-done, bf16[2,512,2048]{2,1,0:T(8,128)(2,1)} %all-gather.5.cloned.1.call-done), kind=kOutput, calls=%fused_computation.10 | convolution fusion | flops 2147483648 | bytes 11534336 | tf_op jit(solution)/shard_map/dot_general | solution.py:54
  280.8 0.0 copy-done.3
  280.9 0.0 copy-done.1
  280.9 5.8 %add_bitcast_fusion = f32[1024,2048]{0,1:T(8,128)} fusion(f32[2048,1024]{1,0:T(8,128)S(1)} %fusion.3, bf16[512,1024]{1,0:T(8,128)(2,1)S(1)} %copy-done.3, bf16[2,512,2048]{2,1,0:T(8,128)(2,1)S(1)} %copy-done.1), kind=kOutput, calls=%fused_computation.1 | convolution fusion | flops 2149580800 | bytes 19922944 | tf_op jit(solution)/shard_map/dot_general | solution.py:57
  286.7 0.0 reduce-scatter.5.cloned.1.call-update
  286.7 80.2 %reduce-scatter.5.cloned.1.call-done = f32[256,2048]{0,1:T(8,128)} async-done(((f32[1024,2048]{0,1:T(8,128)}), f32[256,2048]{0,1:T(8,128)}) %reduce-scatter.5.cloned.1.call-update) | async-done | bytes 2097168 | tf_op jit(solution)/shard_map/reduce_scatter | solution.py:60
  366.9 2.9 copy.8
  (3 shorter events, 0.1 us)
Async XLA Ops:
  6.5 5.0 %copy-start = (bf16[512,1024]{1,0:T(8,128)(2,1)S(1)}, bf16[512,1024]{1,0:T(8,128)(2,1)}, u32[]{:S(2)}) copy-start(bf16[512,1024]{1,0:T(8,128)(2,1)} %param.3) | copy-start | bytes 3145732
  6.5 66.4 %reduce-scatter.3.cloned.1.call-start = ((), (), s32[]{:S(2)}) async-start(), calls=%async_computation.5 | async-start | bytes 9437184 | tf_op jit(solution)/shard_map/reduce_scatter | solution.py:28
  6.5 5.0 %copy-start.4 = (bf16[1024,2048]{1,0:T(8,128)(2,1)S(1)}, bf16[1024,2048]{1,0:T(8,128)(2,1)}, u32[]{:S(2)}) copy-start(bf16[1024,2048]{1,0:T(8,128)(2,1)} %param.5) | copy-start | bytes 12582916
  17.7 148.7 %all-gather.3.cloned.1.call-start = ((), (), s32[]{:S(2)}) async-start(), calls=%async_computation.6 | async-start | bytes 17301504 | tf_op jit(solution)/shard_map/all_gather | solution.py:37
  94.2 83.5 %all-to-all-start.1 = ((f32[32,2,2048]{2,1,0:T(2,128)}), f32[32,2,2048]{2,1,0:T(2,128)S(1)}, u32[]{:S(2)}, u32[]{:S(2)}) async-start(f32[32,2,2048]{2,1,0:T(2,128)} %broadcast_in_dim.10), calls=%async_computation.2 | async-start | bytes 1048576 | tf_op jit(solution)/shard_map/all_to_all | solution.py:11
  180.2 53.6 %all-to-all-start.2 = ((f32[4,2,64,2048]{3,2,1,0:T(8,128)}), f32[4,2,64,2048]{3,2,1,0:T(8,128)}, u32[]{:S(2)}, u32[]{:S(2)}) async-start(f32[4,2,64,2048]{3,2,1,0:T(8,128)} %broadcast_in_dim.12), calls=%async_computation.3 | async-start | bytes 8388608 | tf_op jit(solution)/shard_map/all_to_all | solution.py:11
  185.0 91.7 %all-gather.5.cloned.1.call-start = ((), (), s32[]{:S(2)}) async-start(), calls=%async_computation.7 | async-start | bytes 4718592 | tf_op jit(solution)/shard_map/all_gather | solution.py:52
  186.4 49.9 %copy-start.2 = (f32[1,64,2048]{2,1,0:T(8,128)S(1)}, f32[1,64,2048]{2,1,0:T(8,128)}, u32[]{:S(2)}) copy-start(f32[1,64,2048]{2,1,0:T(8,128)} %get-tuple-element.6) | copy-start | bytes 1572868
  246.1 34.7 %copy-start.3 = (bf16[512,1024]{1,0:T(8,128)(2,1)S(1)}, bf16[512,1024]{1,0:T(8,128)(2,1)}, u32[]{:S(2)}) copy-start(bf16[512,1024]{1,0:T(8,128)(2,1)} %param.4) | copy-start | bytes 3145732
  246.2 120.7 %reduce-scatter.5.cloned.1.call-start = ((), (), s32[]{:S(2)}) async-start(), calls=%async_computation.8 | async-start | bytes 10485760 | tf_op jit(solution)/shard_map/reduce_scatter | solution.py:60
  276.7 4.2 %copy-start.1 = (bf16[2,512,2048]{2,1,0:T(8,128)(2,1)S(1)}, bf16[2,512,2048]{2,1,0:T(8,128)(2,1)}, u32[]{:S(2)}) copy-start(bf16[2,512,2048]{2,1,0:T(8,128)(2,1)} %all-gather.5.cloned.1.call-done) | copy-start | bytes 12582916
Sparse Core Ops, SparseCore 0:
  17.9 55.0 reduce-scatter.2
  93.2 73.2 all-gather.2
  246.3 30.3 all-gather.4
  286.8 80.0 reduce-scatter.4
where the time goes:
time: 377 us; the launch traced here: 376 us
  waiting for transfers between devices  281 us (75%)
  matrix products  38.2 us (10%)
  blocking collectives  17.3 us (5%)
  between operations  13.3 us (4%)
  other arithmetic  10.1 us (3%)
  starting transfers between devices  9.61 us (3%)
  local copies, waits for them, and re-layouts  6.74 us (2%)
    reduce_scatter x1, waiting for transfers between devices, body(): lax.psum_scatter(left_part + right_part, 'crop', scatter_dimension=0, til...  80.2 us
    all_gather x1, waiting for transfers between devices, body(): everyone = lax.all_gather(rounded, ('dp', 'crop'), axis=1, tiled=True)  67.9 us
    reduce_scatter x1, waiting for transfers between devices, body(): lax.psum_scatter(jnp.stack([left_part, right_part], axis=1), 'dp', scatte...  55.2 us
    all_to_all x2, waiting for transfers between devices, sent_to_all(): lax.all_to_all(jnp.broadcast_to(array[None], (peers, *array.shape)), axis...  47.3 us
    all_gather x1, waiting for transfers between devices, body(): block_grads = lax.all_gather(row_grads, 'dp', axis=1, tiled=True)  30.5 us
    all_to_all x1, blocking collectives, sent_to_all(): lax.all_to_all(jnp.broadcast_to(array[None], (peers, *array.shape)), axis...  17.3 us
    dot_general x1, matrix products, body(): jnp.einsum('vrf,vbf->vrb', rounded, everyone, preferred_element_type=jnp....  11.1 us
    dot_general x1, matrix products, body(): jnp.einsum('vrb,vbf->vrf', gram_low, everyone, preferred_element_type=jnp...  9.76 us
  transfers between devices with their start and end apart: 6, of which 5 were waited for; matrix products, arithmetic and copies ran while one was open for 4% of the time, Pallas kernels for 0%

commit v1 on v0

--- a/solution.py
+++ b/solution.py
@@ -2,6 +2,7 @@
 import jax.numpy as jnp
 from jax import lax
 from jax.sharding import PartitionSpec as P
+from jax.lax import all_gather
 
 epsilon = 0.0001
 
@@ -18,6 +19,11 @@
 
 
 def body(hidden_a, hidden_b, weight):
+
+    def build_face(state, k_dim):
+        block_last = all_gather(state, ("dp", "crop"))
+        return jnp.concatenate(block_last, axis=k_dim)
+
     group_size = lax.axis_size(("dp", "crop"))
     data_count = lax.axis_size("dp")
     block_rows = hidden_a.shape[0]
@@ -34,7 +40,7 @@
     spread = over_copies(jnp.sum(centered * centered, axis=1), ("dp", "crop"))
     deviation = jnp.sqrt(spread / (total_rows - 1.0) + epsilon)
     rounded = centered.astype(jnp.bfloat16)
-    everyone = lax.all_gather(rounded, ("dp", "crop"), axis=1, tiled=True)
+    everyone = build_face(rounded, 1)
     gram = jnp.einsum("vrf,vbf->vrb", rounded, everyone, preferred_element_type=jnp.float32)
     gram = over_copies(gram, "tensor")
     gram_low = gram.astype(jnp.bfloat16)

time: 377 us -> 392 us (1.040)
  local copies, waits for them, and re-layouts: 6.74 us -> 22.2 us
    all_gather x0 -> x1, local copies, waits for them, and re-layouts: none -> 14.1 us  [build_face(): block_last = all_gather(state, ('dp', 'crop'))]
  transfers between devices with their start and end apart: 6 -> 6, of which waited for: 5 -> 5; matrix products, arithmetic and copies ran while one was open for 4% -> 7% of each run, Pallas kernels for 0% -> 0%
where the time goes in v1:
time: 392 us; the launch traced here: 391 us
  waiting for transfers between devices  281 us (72%)
  matrix products  37.7 us (10%)
  local copies, waits for them, and re-layouts  22.2 us (6%)
  blocking collectives  17.3 us (4%)
  between operations  13.3 us (3%)
  other arithmetic  10.2 us (3%)
  starting transfers between devices  9.61 us (2%)
    reduce_scatter x1, waiting for transfers between devices, body(): lax.psum_scatter(left_part + right_part, 'crop', scatter_dimension=0, til...  80.2 us
    all_gather x1, waiting for transfers between devices, build_face(): block_last = all_gather(state, ('dp', 'crop'))  67.5 us
    reduce_scatter x1, waiting for transfers between devices, body(): lax.psum_scatter(jnp.stack([left_part, right_part], axis=1), 'dp', scatte...  55.2 us
    all_to_all x2, waiting for transfers between devices, sent_to_all(): lax.all_to_all(jnp.broadcast_to(array[None], (peers, *array.shape)), axis...  47.3 us
    all_gather x1, waiting for transfers between devices, body(): block_grads = lax.all_gather(row_grads, 'dp', axis=1, tiled=True)  30.5 us
    all_to_all x1, blocking collectives, sent_to_all(): lax.all_to_all(jnp.broadcast_to(array[None], (peers, *array.shape)), axis...  17.3 us
    all_gather x1, local copies, waits for them, and re-layouts, build_face(): block_last = all_gather(state, ('dp', 'crop'))  14.1 us
    dot_general x1, matrix products, body(): jnp.einsum('vrf,vbf->vrb', rounded, everyone, preferred_element_type=jnp....  10.9 us
  transfers between devices with their start and end apart: 6, of which 5 were waited for; matrix products, arithmetic and copies ran while one was open for 7% of the time, Pallas kernels for 0%

profile of v1, /device:TPU:1, one launch (start us, length us, event | category | flops | bytes accessed | tf_op | source)
XLA Modules:
  0.0 391.0 jit_solution(15544803667763539559)
XLA Ops:
  6.5 0.0 copy-start
  6.5 0.0 copy-start.3
  6.5 0.0 reduce-scatter.3.cloned.1.call-start
  6.5 1.2 copy-done
  7.8 4.7 %convolution_bitcast_fusion.1 = f32[512,1,2048]{2,0,1:T(8,128)S(1)} fusion(bf16[512,1024]{1,0:T(8,128)(2,1)S(1)} %copy-done, bf16[1024,2048]{1,0:T(8,128)(2,1)} %param.5), kind=kOutput, calls=%fused_computation.3 | convolution fusion | flops 2147483648 | bytes 9437184 | tf_op jit(solution)/shard_map/dot_general | solution.py:32
  12.4 0.0 copy-done.3
  12.4 0.0 copy-done.5
  12.5 2.4 convolution_bitcast_fusion
  14.8 3.8 pad_maximum_fusion
  18.6 0.0 reduce-scatter.3.cloned.1.call-update
  18.7 0.0 all-gather.3.cloned.1.call-start
  18.7 55.2 %reduce-scatter.3.cloned.1.call-done = f32[64,2,2048]{2,0,1:T(8,128)} async-done(((f32[512,2,2048]{2,0,1:T(8,128)}), f32[64,2,2048]{2,0,1:T(8,128)}) %reduce-scatter.3.cloned.1.call-update) | async-done | bytes 1048592 | tf_op jit(solution)/shard_map/reduce_scatter | solution.py:34
  73.9 1.3 convert_element_type.33
  75.2 0.1 slice_bitcast_fusion.7
  75.3 0.1 convert_reduce_fusion
  75.4 0.2 broadcast_in_dim.9
  75.7 17.3 %all_to_all.15 = f32[32,2,2048]{2,1,0:T(2,128)S(1)} all-to-all(f32[32,2,2048]{2,1,0:T(2,128)S(1)} %broadcast_in_dim.9), channel_id=1, replica_groups=mesh['dp'=8,'crop'=4,'tensor'=4] {'dp','crop'}, dimensions={0} | all-to-all | bytes 1048576 | tf_op jit(solution)/shard_map/all_to_all | solution.py:12
  93.0 0.2 reduce_sum.46
  93.1 0.9 subtract_convert_fusion
  94.0 0.0 all-gather.3.cloned.1.call-update
  94.1 0.2 multiply_reduce_fusion
  94.2 1.0 broadcast_in_dim.10
  95.3 4.5 %all-to-all-start.1 = ((f32[32,2,2048]{2,1,0:T(2,128)}), f32[32,2,2048]{2,1,0:T(2,128)S(1)}, u32[]{:S(2)}, u32[]{:S(2)}) async-start(f32[32,2,2048]{2,1,0:T(2,128)} %broadcast_in_dim.10), calls=%async_computation.2 | async-start | bytes 1048576 | tf_op jit(solution)/shard_map/all_to_all | solution.py:12
  99.8 67.5 %all-gather.3.cloned.1.call-done = bf16[32,2,64,2048]{3,2,1,0:T(8,128)(2,1)} async-done(((bf16[1,2,64,2048]{3,2,1,0:T(8,128)(2,1)}), bf16[32,2,64,2048]{3,2,1,0:T(8,128)(2,1)}) %all-gather.3.cloned.1.call-update) | async-done | bytes 16777232 | tf_op jit(solution)/shard_map/all_gather | solution.py:24
  167.3 14.1 %copy.13 = bf16[32,2,64,2048]{3,2,0,1:T(8,128)(2,1)} copy(bf16[32,2,64,2048]{3,2,1,0:T(8,128)(2,1)} %all-gather.3.cloned.1.call-done) | data formatting | bytes 33554432 | tf_op jit(solution)/shard_map/all_gather | solution.py:24
  181.4 10.9 %fusion.5 = f32[2,64,2048]{2,1,0:T(8,128)S(1)} fusion(bf16[2,2048,2048]{2,1,0:T(8,128)(2,1)} %bitcast.32, f32[2,2048]{1,0:T(2,128)S(1)} %broadcast_multiply_fusion, bf16[1,64,2048]{2,1,0:T(8,128)(2,1)S(1)} %get-tuple-element.10, bf16[1,64,2048]{2,1,0:T(8,128)(2,1)S(1)} %get-tuple-element.7), kind=kOutput, calls=%fused_computation.17 | convolution fusion | flops 1074790400 | bytes 18366464 | tf_op jit(solution)/shard_map/vrf,vbf->vrb/dot_general | solution.py:44
  192.3 0.0 all-to-all-done.1
  192.3 2.6 broadcast_in_dim.12
  194.9 4.8 %all-to-all-start.2 = ((f32[4,2,64,2048]{3,2,1,0:T(8,128)}), f32[4,2,64,2048]{3,2,1,0:T(8,128)}, u32[]{:S(2)}, u32[]{:S(2)}) async-start(f32[4,2,64,2048]{3,2,1,0:T(8,128)} %broadcast_in_dim.12), calls=%async_computation.3 | async-start | bytes 8388608 | tf_op jit(solution)/shard_map/all_to_all | solution.py:12
  199.7 0.2 all-gather.5.cloned.1.call-start
  200.0 0.1 fusion.8
  200.1 0.9 fusion.9
  201.0 0.2 reduce_sum.48
  201.2 47.3 %all-to-all-done.2 = f32[4,2,64,2048]{3,2,1,0:T(8,128)} async-done(((f32[4,2,64,2048]{3,2,1,0:T(8,128)}), f32[4,2,64,2048]{3,2,1,0:T(8,128)}, u32[]{:S(2)}, u32[]{:S(2)}) %all-to-all-start.2) | async-done | bytes 4194336 | tf_op jit(solution)/shard_map/all_to_all | solution.py:12
  248.4 2.6 reduce_sum.49
  251.1 0.0 copy-done.2
  251.1 9.8 %fusion.2 = bf16[2,64,2048]{2,1,0:T(8,128)(2,1)} fusion(bf16[2,2048,2048]{2,1,0:T(8,128)(2,1)} %bitcast.33, f32[1,64,2048]{2,1,0:T(8,128)S(1)} %get-tuple-element.5, f32[1,64,2048]{2,1,0:T(8,128)S(1)} %copy-done.2, f32[2,2048]{1,0:T(2,128)S(1)} %reduce_sum.48, bf16[2,64,2048]{2,1,0:T(8,128)(2,1)S(1)} %reduce_sum.49, f32[2,2048]{1,0:T(2,128)S(1)} %compare_select_fusion, ...), kind=kOutput, calls=%fused_computation.7 | convolution fusion | flops 1076887552 | bytes 19447808 | tf_op jit(solution)/shard_map/vrb,vbf->vrf/dot_general | solution.py:47
  260.8 0.0 all-gather.5.cloned.1.call-update
  260.8 0.0 copy-start.4
  260.9 0.0 reduce-scatter.5.cloned.1.call-start
  260.9 30.5 %all-gather.5.cloned.1.call-done = bf16[2,512,2048]{2,1,0:T(8,128)(2,1)} async-done(((bf16[2,64,2048]{2,1,0:T(8,128)(2,1)}), bf16[2,512,2048]{2,1,0:T(8,128)(2,1)}) %all-gather.5.cloned.1.call-update) | async-done | bytes 4194320 | tf_op jit(solution)/shard_map/all_gather | solution.py:58
  291.4 4.1 %fusion.3 = f32[2048,1024]{1,0:T(8,128)S(1)} fusion(bf16[512,1024]{1,0:T(8,128)(2,1)S(1)} %copy-done, bf16[2,512,2048]{2,1,0:T(8,128)(2,1)} %all-gather.5.cloned.1.call-done), kind=kOutput, calls=%fused_computation.10 | convolution fusion | flops 2147483648 | bytes 11534336 | tf_op jit(solution)/shard_map/dot_general | solution.py:60
  295.6 0.0 copy-done.4
  295.6 0.0 copy-done.1
  295.6 5.8 %add_bitcast_fusion = f32[1024,2048]{0,1:T(8,128)} fusion(f32[2048,1024]{1,0:T(8,128)S(1)} %fusion.3, bf16[512,1024]{1,0:T(8,128)(2,1)S(1)} %copy-done.4, bf16[2,512,2048]{2,1,0:T(8,128)(2,1)S(1)} %copy-done.1), kind=kOutput, calls=%fused_computation.1 | convolution fusion | flops 2149580800 | bytes 19922944 | tf_op jit(solution)/shard_map/dot_general | solution.py:63
  301.4 0.0 reduce-scatter.5.cloned.1.call-update
  301.4 80.2 %reduce-scatter.5.cloned.1.call-done = f32[256,2048]{0,1:T(8,128)} async-done(((f32[1024,2048]{0,1:T(8,128)}), f32[256,2048]{0,1:T(8,128)}) %reduce-scatter.5.cloned.1.call-update) | async-done | bytes 2097168 | tf_op jit(solution)/shard_map/reduce_scatter | solution.py:66
  381.6 2.9 copy.14
  (5 shorter events, 0.1 us)
Async XLA Ops:
  6.5 1.2 copy-start
  6.5 5.9 %copy-start.3 = (bf16[512,1024]{1,0:T(8,128)(2,1)S(1)}, bf16[512,1024]{1,0:T(8,128)(2,1)}, u32[]{:S(2)}) copy-start(bf16[512,1024]{1,0:T(8,128)(2,1)} %param.4) | copy-start | bytes 3145732
  6.5 67.4 %reduce-scatter.3.cloned.1.call-start = ((), (), s32[]{:S(2)}) async-start(), calls=%async_computation.5 | async-start | bytes 9437184 | tf_op jit(solution)/shard_map/reduce_scatter | solution.py:34
  7.8 4.7 %copy-start.5 = (bf16[1024,2048]{1,0:T(8,128)(2,1)S(1)}, bf16[1024,2048]{1,0:T(8,128)(2,1)}, u32[]{:S(2)}) copy-start(bf16[1024,2048]{1,0:T(8,128)(2,1)} %param.5) | copy-start | bytes 12582916
  18.7 148.6 %all-gather.3.cloned.1.call-start = ((), (), s32[]{:S(2)}) async-start(), calls=%async_computation.6 | async-start | bytes 17301504 | tf_op jit(solution)/shard_map/all_gather | solution.py:24
  95.3 97.1 %all-to-all-start.1 = ((f32[32,2,2048]{2,1,0:T(2,128)}), f32[32,2,2048]{2,1,0:T(2,128)S(1)}, u32[]{:S(2)}, u32[]{:S(2)}) async-start(f32[32,2,2048]{2,1,0:T(2,128)} %broadcast_in_dim.10), calls=%async_computation.2 | async-start | bytes 1048576 | tf_op jit(solution)/shard_map/all_to_all | solution.py:12
  194.9 53.5 %all-to-all-start.2 = ((f32[4,2,64,2048]{3,2,1,0:T(8,128)}), f32[4,2,64,2048]{3,2,1,0:T(8,128)}, u32[]{:S(2)}, u32[]{:S(2)}) async-start(f32[4,2,64,2048]{3,2,1,0:T(8,128)} %broadcast_in_dim.12), calls=%async_computation.3 | async-start | bytes 8388608 | tf_op jit(solution)/shard_map/all_to_all | solution.py:12
  199.7 91.7 %all-gather.5.cloned.1.call-start = ((), (), s32[]{:S(2)}) async-start(), calls=%async_computation.7 | async-start | bytes 4718592 | tf_op jit(solution)/shard_map/all_gather | solution.py:58
  201.1 49.9 %copy-start.2 = (f32[1,64,2048]{2,1,0:T(8,128)S(1)}, f32[1,64,2048]{2,1,0:T(8,128)}, u32[]{:S(2)}) copy-start(f32[1,64,2048]{2,1,0:T(8,128)} %get-tuple-element.6) | copy-start | bytes 1572868
  260.8 34.7 %copy-start.4 = (bf16[512,1024]{1,0:T(8,128)(2,1)S(1)}, bf16[512,1024]{1,0:T(8,128)(2,1)}, u32[]{:S(2)}) copy-start(bf16[512,1024]{1,0:T(8,128)(2,1)} %param.4) | copy-start | bytes 3145732
  260.9 120.8 %reduce-scatter.5.cloned.1.call-start = ((), (), s32[]{:S(2)}) async-start(), calls=%async_computation.8 | async-start | bytes 10485760 | tf_op jit(solution)/shard_map/reduce_scatter | solution.py:66
  291.4 4.2 %copy-start.1 = (bf16[2,512,2048]{2,1,0:T(8,128)(2,1)S(1)}, bf16[2,512,2048]{2,1,0:T(8,128)(2,1)}, u32[]{:S(2)}) copy-start(bf16[2,512,2048]{2,1,0:T(8,128)(2,1)} %all-gather.5.cloned.1.call-done) | copy-start | bytes 12582916
Sparse Core Ops, SparseCore 0:
  18.8 55.0 reduce-scatter.2
  94.2 73.0 all-gather.2
  261.0 30.3 all-gather.4
  301.5 80.0 reduce-scatter.4
